TPU v7x, 32 devices: a whole 2x2x4 slice. The times are simulated.
32 devices in a mesh: kpt: 4 (over y, x), pw: 8 (over z, core).
Axes of the slice: x: 2, y: 2, z: 4, core: 2. Of those that a mesh axis runs over, the one named last changes fastest.
Arguments:
- energies: float32 [16, 512], P('kpt', 'pw'), may hold values from 0.5 to 3
- current: float32 [2, 16, 512], P(None, 'kpt', 'pw'), may hold values from -40 to 40
- previous: float32 [2, 16, 512], P(None, 'kpt', 'pw'), may hold values from -6 to 6
- previous_beta: float32 [2], replicated, may hold values from 0.5 to 2
- pair_left: bfloat16 [16, 512, 4096], P('kpt', None, 'pw'), may hold values from -0.09375 to 0.09375
- pair_right: bfloat16 [16, 512, 4096], P('kpt', None, 'pw'), may hold values from -0.25 to 0.25
- screened: bfloat16 [16, 4096, 4096], P('kpt', 'pw'), may hold values from -0.0234375 to 0.0234375
- momentum_index: int32 [16, 16], replicated, may hold values from 0 to 15, each once within a row
Outputs:
- last_vector: float32 [2, 16, 512], P(None, 'kpt', 'pw')
- prior_vector: float32 [2, 16, 512], P(None, 'kpt', 'pw')
- alpha_terms: float32 [2, 3], replicated
- beta_terms: float32 [2, 3], replicated
Inputs may be any that keep to these rules, and one draw needn't show every extreme that they name: Each row of momentum_index names every index from 0 to 15 once.
All inputs are finite; a program needn't handle non-finite values.
Results may differ from a plain program's by a relative error of at most 0.003.
Values may be sent and summed in bfloat16 or wider, within the bound.
A program may use at most 128 MiB of HBM per device.

v0:
```python
import functools

import jax
import jax.numpy as jnp
from jax import lax
from jax.experimental import pallas as pl
from jax.experimental.pallas import tpu as pltpu
from jax.sharding import PartitionSpec as P

STEPS = 3
LANES = 128

epsilon = 1e-06


def partner(me, i, n):
    i = jnp.int32(i)
    out = jnp.int32(0)
    bit = 1
    while bit < n:
        out = out + lax.rem(lax.div(me, bit) + lax.div(i, bit), 2) * bit
        bit *= 2
    return out


def exchange(buf, axis, n, me, i, send_sem, recv_sem, src=None):
    return pltpu.make_async_remote_copy(
        src_ref=buf.at[me] if src is None else src,
        dst_ref=buf.at[me],
        send_sem=send_sem.at[i],
        recv_sem=recv_sem.at[i],
        device_id={axis: partner(me, i, n)},
        device_id_type=pl.DeviceIdType.MESH,
    )


def arrival(buf, axis, n, me, i, send_sem, recv_sem):
    slot = partner(me, i, n)
    return pltpu.make_async_remote_copy(
        src_ref=buf.at[slot],
        dst_ref=buf.at[slot],
        send_sem=send_sem.at[i],
        recv_sem=recv_sem.at[i],
        device_id={axis: slot},
        device_id_type=pl.DeviceIdType.MESH,
    )


def kernel(
    dims,
    energies_ref, current_ref, previous_ref, beta_ref, index_ref,
    right_hbm, left_hbm, screened_hbm,
    last_ref, prior_ref, alphas_ref, betas_ref,
    right, left, screened, packs, first, later, final, dens, held, fields, directs,
    dfull, vec_ref, early_ref, coef_ref, applied_ref, energy_ref, choose_ref, acc,
    right_sem, left_sem, screened_sem,
    pack_s, pack_r, full_s, full_r, kdens_s, kdens_r, gdens_s, gdens_r, field_s, field_r,
    direct_s, direct_r, final_s, final_r,
):
    nkp, npw, kl, nv, bands, gs = dims
    rows = kl * nv
    total = rows * nkp
    entries = total // nv * bands
    kme = lax.axis_index("kpt")
    pme = lax.axis_index("pw")

    right_copy = pltpu.make_async_copy(right_hbm, right, right_sem)
    left_copy = pltpu.make_async_copy(left_hbm, left, left_sem)

    def screened_copy(i):
        chunk = partner(pme, i, npw)
        start = pl.multiple_of(chunk * gs, gs)
        return pltpu.make_async_copy(
            screened_hbm.at[:, :, pl.ds(start, gs)], screened.at[chunk], screened_sem.at[i]
        )

    right_copy.start()
    for i in range(npw):
        screened_copy(i).start()
    left_copy.start()

    barrier = pltpu.get_barrier_semaphore()
    for axis, n, me in (("kpt", nkp, kme), ("pw", npw, pme)):
        for i in range(1, n):
            pl.semaphore_signal(
                barrier, inc=1, device_id={axis: partner(me, i, n)},
                device_id_type=pl.DeviceIdType.MESH,
            )
    width = energies_ref.shape[1]
    per = LANES // width
    levels = energies_ref[...]
    block = jnp.concatenate(
        [current_ref[v] for v in range(nv)]
        + [previous_ref[v] for v in range(nv)]
        + [levels for v in range(nv)],
        axis=0,
    )
    turn_at = lax.rem(pme, per)
    packs[pme] = jnp.concatenate(
        [block * (turn_at == j).astype(jnp.float32) for j in range(per)], axis=1
    )
    pl.semaphore_wait(barrier, nkp - 1 + npw - 1)

    pending = []

    def send_all(buf, axis, n, me, ssem, rsem):
        for i in range(1, n):
            copy = exchange(buf, axis, n, me, i, ssem, rsem)
            copy.start()
            pending.append(copy)

    def wait_all(buf, axis, n, me, ssem, rsem):
        for i in range(1, n):
            arrival(buf, axis, n, me, i, ssem, rsem).wait_recv()

    send_all(packs, "pw", npw, pme, pack_s, pack_r)

    points = nkp * kl
    row = lax.broadcasted_iota(jnp.int32, (total, points), 0)
    col = lax.broadcasted_iota(jnp.int32, (total, points), 1)
    point = (row // rows) * kl + lax.rem(row, kl)
    spread = (point == col).astype(jnp.bfloat16)
    index = index_ref[...].astype(jnp.float32).astype(jnp.bfloat16)
    wide = jnp.dot(spread, index, preferred_element_type=jnp.float32).astype(jnp.bfloat16)
    wide = lax.dot_general(
        wide, spread, (((1,), (1,)), ((), ())), preferred_element_type=jnp.float32
    )
    chain_row = lax.rem(lax.broadcasted_iota(jnp.int32, (total, total), 0), rows) // kl
    chain_col = lax.rem(lax.broadcasted_iota(jnp.int32, (total, total), 1), rows) // kl
    same = (chain_row == chain_col).astype(jnp.float32)
    for q in range(kl):
        transfer = (kme * kl + q).astype(jnp.float32)
        choose_ref[q * total : (q + 1) * total, :] = (
            same * jnp.maximum(1.0 - jnp.abs(wide - transfer), 0.0)
        ).astype(jnp.bfloat16)

    wait_all(packs, "pw", npw, pme, pack_s, pack_r)

    whole = jnp.concatenate(
        [sum(packs[m * per + j] for j in range(per)) for m in range(bands // LANES)], axis=1
    )
    vec_ref[...] = whole[:rows]
    early_ref[...] = whole[rows : 2 * rows]
    energy_ref[...] = whole[2 * rows :]
    coef_ref[...] = jnp.zeros_like(coef_ref)

    row_g = lax.broadcasted_iota(jnp.int32, (rows, gs), 0)
    row_g = lax.rem(row_g, kl)
    row_c = lax.rem(lax.broadcasted_iota(jnp.int32, (rows, bands), 0), kl)
    row_v = lax.broadcasted_iota(jnp.int32, (rows, LANES), 0) // kl
    lane = lax.broadcasted_iota(jnp.int32, (rows, LANES), 1)

    def densities(x):
        high = x.astype(jnp.bfloat16).astype(jnp.float32)
        both = jnp.concatenate([high, x - high], axis=0).astype(jnp.bfloat16)
        top = jnp.zeros((rows, gs), jnp.float32)
        low = jnp.zeros((rows, gs), jnp.float32)
        for k in range(kl):
            res = jnp.dot(both, right[k], preferred_element_type=jnp.float32)
            top = jnp.where(row_g == k, res[:rows], top)
            low = jnp.where(row_g == k, res[rows:], low)
        return top, low

    def sums_tile(vec, applied):
        cross = jnp.sum(vec * applied, axis=1, keepdims=True)
        square = jnp.sum(applied * applied, axis=1, keepdims=True)
        own = jnp.sum(vec * vec, axis=1, keepdims=True)
        return jnp.where(lane == 0, cross, jnp.where(lane == 1, square, own))

    def coefficients(tile, turn):
        sums = jnp.zeros_like(tile)
        for v in range(nv):
            chain = jnp.sum(jnp.where(row_v == v, tile, 0.0), axis=0, keepdims=True)
            sums = jnp.where(row_v == v, chain, sums)
        alpha = sums[:, 0:1] / entries
        mean = sums[:, 1:2] / entries - 2.0 * alpha * alpha + alpha * alpha * (sums[:, 2:3] / entries)
        beta = jnp.sqrt(mean + epsilon)
        coef = jnp.where(lane == turn, alpha, coef_ref[...])
        coef_ref[...] = jnp.where(lane == STEPS + turn, beta, coef)
        return alpha, beta

    def advance(alpha, beta):
        vec = vec_ref[...]
        early_ref[...] = vec
        vec_ref[...] = (applied_ref[...] - alpha * vec) / beta

    beta_before = jnp.zeros((rows, 1), jnp.float32)
    for v in range(nv):
        beta_before = jnp.where(row_v[:, 0:1] == v, beta_ref[v], beta_before)
    right_copy.wait()
    for turn in range(STEPS):
        if turn == 0:
            top, low = densities(vec_ref[...])
            first[kme] = top.astype(jnp.bfloat16)
            send_all(first, "kpt", nkp, kme, kdens_s.at[turn], kdens_r.at[turn])
            dfull[kme] = top + low
            wait_all(first, "kpt", nkp, kme, kdens_s.at[turn], kdens_r.at[turn])
            blocks = [first[s].astype(jnp.float32) for s in range(nkp)]
        else:
            applied = applied_ref[...]
            top, low = densities(applied)
            mine = later.at[turn - 1]
            mine[kme] = jnp.concatenate([top + low, sums_tile(vec_ref[...], applied)], axis=1)
            send_all(mine, "kpt", nkp, kme, kdens_s.at[turn], kdens_r.at[turn])
            wait_all(mine, "kpt", nkp, kme, kdens_s.at[turn], kdens_r.at[turn])
            if turn == 1:
                wait_all(dfull, "kpt", nkp, kme, full_s, full_r)
                for copy in full_copies:
                    copy.wait_send()
            alpha, beta = coefficients(sum(mine[s][:, gs:] for s in range(nkp)), turn - 1)
            blocks = []
            for s in range(nkp):
                block = (mine[s][:, :gs] - alpha * dfull[s]) / beta
                dfull[s] = block
                blocks.append(block)
        gathered = dens.at[turn]
        gathered[pme] = jnp.concatenate(blocks, axis=0).astype(jnp.bfloat16)
        gsend, grecv = gdens_s.at[turn], gdens_r.at[turn]
        for i in [1] + list(range(2, npw, 2)):
            copy = exchange(gathered, "pw", npw, pme, i, gsend, grecv)
            copy.start()
            pending.append(copy)
        if turn == 0:
            full_copies = []
            for i in range(1, nkp):
                copy = exchange(dfull, "kpt", nkp, kme, i, full_s, full_r)
                copy.start()
                full_copies.append(copy)
        if turn > 0:
            advance(alpha, beta)
            beta_before = beta
        acc[...] = jnp.zeros_like(acc)

        def product(i):
            if turn == 0:
                screened_copy(i).wait()
            chunk = partner(pme, i, npw)
            picked = jnp.dot(
                choose_ref[...], gathered[chunk], preferred_element_type=jnp.float32
            ).astype(jnp.bfloat16)
            part = acc[...]
            for q in range(kl):
                part = part + lax.dot_general(
                    picked[q * total : (q + 1) * total],
                    screened[chunk, q],
                    (((1,), (1,)), ((), ())),
                    preferred_element_type=jnp.float32,
                )
            acc[...] = part

        def forward(i):
            slot = partner(pme, i, npw)
            return pltpu.make_async_remote_copy(
                src_ref=gathered.at[slot],
                dst_ref=gathered.at[slot],
                send_sem=gsend.at[i + 1],
                recv_sem=grecv.at[i + 1],
                device_id={"pw": partner(pme, 1, npw)},
                device_id_type=pl.DeviceIdType.MESH,
            )

        def near_step(p, carry):
            i = 2 * p
            arrival(gathered, "pw", npw, pme, i, gsend, grecv).wait_recv()
            forward(i).start()
            product(i)
            return carry

        def far_step(p, carry):
            i = 2 * p + 1
            arrival(gathered, "pw", npw, pme, i, gsend, grecv).wait_recv()
            product(i)
            return carry

        product(0)
        far_step(0, 0)
        lax.fori_loop(1, npw // 2, near_step, 0)
        lax.fori_loop(1, npw // 2, far_step, 0)
        pending += [forward(i) for i in range(2, npw, 2)]
        out = held.at[turn]
        for s in range(nkp):
            out[s] = acc[s * rows : (s + 1) * rows, :].astype(jnp.bfloat16)
        mine = fields.at[turn]
        for i in range(1, nkp):
            copy = exchange(
                mine, "kpt", nkp, kme, i, field_s.at[turn], field_r.at[turn],
                src=out.at[partner(kme, i, nkp)],
            )
            copy.start()
            pending.append(copy)
        mine[kme] = out[kme]
        if turn == 0:
            left_copy.wait()
        wait_all(mine, "kpt", nkp, kme, field_s.at[turn], field_r.at[turn])
        field = sum(mine[s].astype(jnp.float32) for s in range(nkp)).astype(jnp.bfloat16)
        part = jnp.zeros((rows, bands), jnp.float32)
        for k in range(kl):
            res = lax.dot_general(
                field, left[k], (((1,), (1,)), ((), ())), preferred_element_type=jnp.float32
            )
            part = jnp.where(row_c == k, res, part)
        mine = directs.at[turn]
        mine[pme] = part.astype(jnp.bfloat16)
        send_all(mine, "pw", npw, pme, direct_s.at[turn], direct_r.at[turn])
        wait_all(mine, "pw", npw, pme, direct_s.at[turn], direct_r.at[turn])
        direct = sum(mine[s].astype(jnp.float32) for s in range(npw))
        applied_ref[...] = (
            energy_ref[...] * vec_ref[...] - direct - beta_before * early_ref[...]
        )
    final[kme] = sums_tile(vec_ref[...], applied_ref[...])
    send_all(final, "kpt", nkp, kme, final_s, final_r)
    wait_all(final, "kpt", nkp, kme, final_s, final_r)
    alpha, beta = coefficients(sum(final[s] for s in range(nkp)), STEPS - 1)
    advance(alpha, beta)
    for source, target in ((vec_ref, last_ref), (early_ref, prior_ref)):
        own = jnp.zeros((rows, width), jnp.float32)
        for m in range(npw):
            own = jnp.where(pme == m, source[:, m * width : (m + 1) * width], own)
        for v in range(nv):
            target[v] = own[v * kl : (v + 1) * kl]
    for v in range(nv):
        alphas_ref[v : v + 1, :] = coef_ref[v * kl : v * kl + 1, :STEPS]
        betas_ref[v : v + 1, :] = coef_ref[v * kl : v * kl + 1, STEPS : 2 * STEPS]
    for copy in pending:
        copy.wait_send()


def on_device(
    nkp, npw,
    energies, current, previous, previous_beta, pair_left, pair_right, screened, momentum_index
):
    nv, kl, width = current.shape
    bands = pair_left.shape[1]
    gs = pair_left.shape[2]
    qcount = screened.shape[0]
    rows = kl * nv
    total = rows * nkp
    f32, bf16 = jnp.float32, jnp.bfloat16
    vmem = pl.BlockSpec(memory_space=pltpu.VMEM)
    hbm = pl.BlockSpec(memory_space=pltpu.HBM)
    smem = pl.BlockSpec(memory_space=pltpu.SMEM)
    dma = pltpu.SemaphoreType.DMA
    return pl.pallas_call(
        functools.partial(kernel, (nkp, npw, kl, nv, bands, gs)),
        out_shape=(
            jax.ShapeDtypeStruct(current.shape, f32),
            jax.ShapeDtypeStruct(current.shape, f32),
            jax.ShapeDtypeStruct((nv, STEPS), f32),
            jax.ShapeDtypeStruct((nv, STEPS), f32),
        ),
        in_specs=[vmem, vmem, vmem, smem, vmem, hbm, hbm, hbm],
        out_specs=(vmem, vmem, vmem, vmem),
        scratch_shapes=[
            pltpu.VMEM((kl, bands, gs), bf16),
            pltpu.VMEM((kl, bands, gs), bf16),
            pltpu.VMEM((npw, qcount, gs, gs), bf16),
            pltpu.VMEM((npw, 3 * rows, LANES), f32),
            pltpu.VMEM((nkp, rows, gs), bf16),
            pltpu.VMEM((STEPS - 1, nkp, rows, gs + LANES), f32),
            pltpu.VMEM((nkp, rows, LANES), f32),
            pltpu.VMEM((STEPS, npw, total, gs), bf16),
            pltpu.VMEM((STEPS, nkp, rows, gs), bf16),
            pltpu.VMEM((STEPS, nkp, rows, gs), bf16),
            pltpu.VMEM((STEPS, npw, rows, bands), bf16),
            pltpu.VMEM((nkp, rows, gs), f32),
            pltpu.VMEM((rows, bands), f32),
            pltpu.VMEM((rows, bands), f32),
            pltpu.VMEM((rows, LANES), f32),
            pltpu.VMEM((rows, bands), f32),
            pltpu.VMEM((rows, bands), f32),
            pltpu.VMEM((qcount * total, total), bf16),
            pltpu.VMEM((total, gs), f32),
            dma, dma, dma((npw,)),
            dma((npw,)), dma((npw,)),
            dma((nkp,)), dma((nkp,)),
            dma((STEPS, nkp)), dma((STEPS, nkp)),
            dma((STEPS, npw)), dma((STEPS, npw)),
            dma((STEPS, nkp)), dma((STEPS, nkp)),
            dma((STEPS, npw)), dma((STEPS, npw)),
            dma((nkp,)), dma((nkp,)),
        ],
        compiler_params=pltpu.CompilerParams(
            collective_id=0, has_side_effects=True, vmem_limit_bytes=60 * 1024 * 1024
        ),
    )(
        energies, current, previous, previous_beta, momentum_index,
        pair_right, pair_left, screened,
    )


def solution(mesh):
    return jax.shard_map(
        functools.partial(on_device, mesh.shape["kpt"], mesh.shape["pw"]),
        mesh=mesh,
        in_specs=(
            P("kpt", "pw"),
            P(None, "kpt", "pw"),
            P(None, "kpt", "pw"),
            P(),
            P("kpt", None, "pw"),
            P("kpt", None, "pw"),
            P("kpt", "pw", None),
            P(),
        ),
        out_specs=(P(None, "kpt", "pw"), P(None, "kpt", "pw"), P(), P()),
        check_vma=False,
    )
```

profile of v0, /device:TPU:0, one launch (start us, length us, event | category | flops | bytes accessed | tf_op | source)
XLA Modules:
  0.0 80.8 jit_solution(1337853641690010147)
XLA Ops:
  0.6 75.2 %shard_map.111 = (f32[2,4,64]{2,1,0:T(4,128)}, f32[2,4,64]{2,1,0:T(4,128)}, f32[2,3]{1,0:T(2,128)}, f32[2,3]{1,0:T(2,128)}) custom-call(f32[4,64]{1,0:T(4,128)} %energies_ref.1, f32[2,4,64]{2,1,0:T(4,128)} %current_ref.1, f32[2,4,64]{2,1,0:T(4,128)} %previous_ref.1, f32[2]{0:T(128)} %beta_ref.1, s32[16,16]{1,0:T(8,128)} %index_ref.1, ...), custom_call_target="tpu_custom_call" | custom-call | tf_op jit(solution)/shard_map/pallas_call | solution.py:343
  75.8 1.3 %copy.16 = f32[2,4,64]{2,1,0:T(4,128)} copy(f32[2,4,64]{2,1,0:T(4,128)} %get-tuple-element.8) | data formatting | bytes 4096
  77.1 1.3 %copy.17 = f32[2,4,64]{2,1,0:T(4,128)} copy(f32[2,4,64]{2,1,0:T(4,128)} %get-tuple-element.9) | data formatting | bytes 4096
  78.3 1.2 %copy.18 = f32[2,3]{1,0:T(2,128)} copy(f32[2,3]{1,0:T(2,128)} %get-tuple-element.10) | data formatting | bytes 48
  79.6 1.2 %copy.19 = f32[2,3]{1,0:T(2,128)} copy(f32[2,3]{1,0:T(2,128)} %get-tuple-element.11) | data formatting | bytes 48
where the time goes:
time: 81.1 us; the launch traced here: 80.8 us
  Pallas kernels  75.2 us (93%)
  local copies, waits for them, and re-layouts  4.95 us (6%)
    pallas_call x1, Pallas kernels, on_device(): pl.pallas_call(functools.partial(kernel, (nkp, npw, kl, nv, bands, gs)),...  75.2 us
    unnamed x4, local copies, waits for them, and re-layouts  4.95 us

commit v1 on v0

v1 whole, which is shorter than its diff:
```python
import functools

import jax
import jax.numpy as jnp
from jax import lax
from jax.experimental import pallas as pl
from jax.experimental.pallas import tpu as pltpu
from jax.sharding import PartitionSpec as P

STEPS = 3
LANES = 128

epsilon = 1e-06


def mark(name):
    pass


def partner(me, i, n):
    i = jnp.int32(i)
    out = jnp.int32(0)
    bit = 1
    while bit < n:
        out = out + lax.rem(lax.div(me, bit) + lax.div(i, bit), 2) * bit
        bit *= 2
    return out


def kernel(
    dims,
    energies_hbm, current_hbm, previous_hbm, beta_hbm, index_hbm,
    right_hbm, left_hbm, screened_hbm,
    result_ref,
    energies, current, previous, beta_in, index,
    right, left, screened, starts, packs, dens, held, fields, directs, sums,
    select, acc,
    small_sem, right_sem, left_sem, screened_sem,
    start_s, start_r, pack_s, pack_r, dens_s, line_r, chunk_r, field_s, field_r,
    direct_s, direct_r, sums_s, sums_r,
):
    nkp, npw, kl, nv, bands, gs = dims
    rows = kl * nv
    total = rows * nkp
    entries = total // nv * bands
    points = nkp * kl
    f32, bf16 = jnp.float32, jnp.bfloat16
    kme = lax.axis_index("kpt")
    pme = lax.axis_index("pw")

    def send(src, dst, i, j, ssem, rsem):
        device = {}
        if i:
            device["kpt"] = partner(kme, i, nkp)
        if j:
            device["pw"] = partner(pme, j, npw)
        pltpu.make_async_remote_copy(
            src_ref=src, dst_ref=dst, send_sem=ssem, recv_sem=rsem,
            device_id=device, device_id_type=pl.DeviceIdType.MESH,
        ).start()

    def bytes_of(ref, ssem, rsem):
        return pltpu.make_async_remote_copy(
            src_ref=ref, dst_ref=ref, send_sem=ssem, recv_sem=rsem,
            device_id={"pw": partner(pme, 1, npw)}, device_id_type=pl.DeviceIdType.MESH,
        )

    def arrived(ref, ssem, rsem):
        bytes_of(ref, ssem, rsem).wait_recv()

    pending = []

    small = [
        pltpu.make_async_copy(source, target, small_sem.at[n])
        for n, (source, target) in enumerate((
            (current_hbm, current), (previous_hbm, previous), (energies_hbm, energies),
            (beta_hbm, beta_in), (index_hbm, index),
        ))
    ]
    right_copy = pltpu.make_async_copy(right_hbm, right, right_sem)
    left_copy = pltpu.make_async_copy(left_hbm, left, left_sem)

    def screened_copy(j):
        first = pl.multiple_of(partner(pme, j, npw) * gs, gs)
        return pltpu.make_async_copy(
            screened_hbm.at[:, :, pl.ds(first, gs)], screened.at[j], screened_sem.at[j]
        )

    mark("start")
    for copy in small:
        copy.start()
    barrier = pltpu.get_barrier_semaphore()
    greet = [(0, j) for j in range(npw - 1, 0, -1)]
    greet += [(i, b) for i in range(nkp - 1, 0, -1) for b in range(2)]
    for i, j in greet:
        device = {"kpt": partner(kme, i, nkp), "pw": partner(pme, j, npw)}
        pl.semaphore_signal(
            barrier, inc=1, device_id=device, device_id_type=pl.DeviceIdType.MESH
        )
    right_copy.start()
    for j in range(npw):
        screened_copy(j).start()
    left_copy.start()

    width = energies.shape[1]
    per = LANES // width
    turn_at = lax.rem(pme, per)

    def spread_lanes(block):
        return jnp.concatenate(
            [block * (turn_at == j).astype(f32) for j in range(per)], axis=1
        )

    small[0].wait()
    own_current = jnp.concatenate([current[v] for v in range(nv)], axis=0)
    starts[0] = spread_lanes(own_current).astype(bf16)
    mark("barrier")
    pl.semaphore_wait(barrier, len(greet))
    mark("startsend")
    for j in range(npw - 1, 0, -1):
        send(starts.at[0], starts.at[j], 0, j, start_s, start_r)
    pending.append(bytes_of(starts.at[pl.ds(1, npw - 1)], start_s, start_r))
    small[1].wait()
    small[2].wait()
    own_levels = energies[...]
    packs[0] = spread_lanes(jnp.concatenate(
        [own_current] + [previous[v] for v in range(nv)] + [own_levels] * nv, axis=0
    ))
    for j in range(npw - 1, 0, -1):
        send(packs.at[0], packs.at[j], 0, j, pack_s, pack_r)
    pending.append(bytes_of(packs.at[pl.ds(1, npw - 1)], pack_s, pack_r))

    small[4].wait()
    wide = kl * total

    def points_of(shape):
        row = lax.rem(lax.broadcasted_iota(jnp.int32, shape, 0), total)
        base = jnp.zeros(shape, jnp.int32)
        for i in range(nkp):
            base = jnp.where(row // rows == i, partner(kme, i, nkp) * kl, base)
        col = lax.broadcasted_iota(jnp.int32, shape, 1)
        return (base + lax.rem(row, kl) == col).astype(bf16)

    table = index[...].astype(f32).astype(bf16)
    pairs = jnp.dot(points_of((total, points)), table, preferred_element_type=f32).astype(bf16)
    pairs = lax.dot_general(
        pairs, points_of((wide, points)), (((1,), (1,)), ((), ())), preferred_element_type=f32
    )
    col = lax.broadcasted_iota(jnp.int32, (total, wide), 1)
    row = lax.broadcasted_iota(jnp.int32, (total, wide), 0)
    transfer = (kme * kl + col // total).astype(f32)
    same = (lax.rem(row, rows) // kl == lax.rem(col, rows) // kl).astype(f32)
    pick = (same * jnp.maximum(1.0 - jnp.abs(pairs - transfer), 0.0)).astype(bf16)
    select[...] = jnp.concatenate([pick, pick], axis=1)

    row_g = lax.rem(lax.broadcasted_iota(jnp.int32, (rows, gs), 0), kl)
    row_c = lax.rem(lax.broadcasted_iota(jnp.int32, (rows, bands), 0), kl)
    row_v = lax.broadcasted_iota(jnp.int32, (rows, LANES), 0) // kl
    lane = lax.broadcasted_iota(jnp.int32, (rows, LANES), 1)

    def joined(buf, part):
        tiles = []
        for m in range(bands // LANES):
            slots = [buf[partner(pme, m * per + j, npw)].astype(f32) for j in range(per)]
            tiles.append(sum(slots))
        return jnp.concatenate(tiles, axis=1)

    def density(x, split):
        high = x.astype(bf16)
        both = high
        if split:
            high = high.astype(f32)
            both = jnp.concatenate([high, x - high], axis=0).astype(bf16)
        out = jnp.zeros((rows, gs), f32)
        for k in range(kl):
            res = jnp.dot(both, right[k], preferred_element_type=f32)
            if split:
                res = res[:rows] + res[rows:]
            out = jnp.where(row_g == k, res, out)
        return out.astype(bf16)

    def tile_of(columns):
        tile = jnp.zeros((rows, LANES), f32)
        for n, column in enumerate(columns):
            tile = jnp.where(lane == n, jnp.sum(column, axis=1, keepdims=True), tile)
        return tile

    def share_sums(step, columns):
        buf = sums.at[step]
        buf[0] = tile_of(columns)
        for i in range(nkp - 1, 0, -1):
            send(buf.at[0], buf.at[i], i, 0, sums_s.at[step], sums_r.at[step])
        pending.append(bytes_of(buf.at[pl.ds(1, nkp - 1)], sums_s.at[step], sums_r.at[step]))

    def take_sums(step, count):
        buf = sums.at[step]
        arrived(buf.at[pl.ds(1, nkp - 1)], sums_s.at[step], sums_r.at[step])
        tile = sum(buf[partner(kme, s, nkp)] for s in range(nkp))
        out = jnp.zeros_like(tile)
        for v in range(nv):
            chain = jnp.sum(jnp.where(row_v == v, tile, 0.0), axis=0, keepdims=True)
            out = jnp.where(row_v == v, chain, out)
        return [out[:, n : n + 1] * (1.0 / entries) for n in range(count)]

    def scalars(uv, uu, vv, sigma):
        gamma = uv + sigma * (vv - 1.0)
        beta = jnp.sqrt(uu - 2.0 * gamma * uv + gamma * gamma * vv + epsilon)
        return gamma, beta

    coef = jnp.zeros((rows, LANES), f32)
    mark("startwait")
    arrived(starts.at[pl.ds(1, npw - 1)], start_s, start_r)
    mark("rightwait")
    right_copy.wait()
    x = joined(starts, rows)
    vec = early = levels = base = image = sigma = unit = None
    for turn in range(STEPS):
        mark(f"dens{turn}")
        gather = dens.at[turn]
        gather[0] = density(x, turn > 0)
        gsend = dens_s.at[turn]
        for j in range(npw - 2, 0, -2):
            send(gather.at[0], gather.at[j * nkp], 0, j, gsend, line_r.at[turn, j // 2])
        for i in range(nkp - 1, 0, -1):
            for b in range(2):
                send(gather.at[0], gather.at[b * nkp + i], i, b, gsend, chunk_r.at[turn, b])
        send(gather.at[0], gather.at[nkp], 0, 1, gsend, chunk_r.at[turn, 1])
        pending.append(bytes_of(gather.at[pl.ds(1, npw * nkp - 1)], gsend, chunk_r.at[turn, 0]))
        if turn > 0:
            mark(f"sums{turn}")
            share_sums(turn, [
                x * vec, x * x, vec * vec, levels * x * x, levels * x * vec, levels * vec * vec
            ])
        mark(f"relay{turn}")
        for j in range(2, npw, 2):
            arrived(gather.at[j * nkp], gsend, line_r.at[turn, j // 2])
            for i in range(nkp - 1, 0, -1):
                for b in range(2):
                    send(
                        gather.at[j * nkp], gather.at[(j + b) * nkp + i], i, b,
                        gsend, chunk_r.at[turn, j + b],
                    )
            send(gather.at[j * nkp], gather.at[(j + 1) * nkp], 0, 1, gsend, chunk_r.at[turn, j + 1])
        if turn == 0:
            mark("packwait")
            arrived(packs.at[pl.ds(1, npw - 1)], pack_s, pack_r)
            whole = joined(packs, 3 * rows)
            vec = whole[:rows]
            early = whole[rows : 2 * rows]
            levels = whole[2 * rows :]
            share_sums(0, [levels * vec * vec, vec * early])
        for j in range(0, npw, 2):
            mark(f"chunkwait{turn}_{j}")
            arrived(gather.at[pl.ds(j * nkp + 1, nkp - 1)], gsend, chunk_r.at[turn, j])
            arrived(gather.at[pl.ds((j + 1) * nkp, nkp)], gsend, chunk_r.at[turn, j + 1])
            if turn == 0:
                screened_copy(j).wait()
                screened_copy(j + 1).wait()
            mark(f"prod{turn}_{j}")
            left_sides = [
                gather[(j + b) * nkp : (j + b + 1) * nkp].reshape(total, gs) for b in range(2)
            ]
            for q in range(kl):
                part = sum(
                    lax.dot_general(
                        left_sides[b], screened[j + b, q],
                        (((1,), (1,)), ((), ())), preferred_element_type=f32,
                    )
                    for b in range(2)
                )
                if j:
                    part = part + acc[q * total : (q + 1) * total]
                acc[q * total : (q + 1) * total] = part
        mark(f"select{turn}")
        images = acc[...]
        high = images.astype(bf16)
        low = (images - high.astype(f32)).astype(bf16)
        out = jnp.dot(
            select[...], jnp.concatenate([high, low], axis=0), preferred_element_type=f32
        )
        for i in range(nkp - 1, 0, -1):
            held[turn, i] = out[i * rows : (i + 1) * rows].astype(bf16)
            send(
                held.at[turn, i], fields.at[turn, i], i, 0, field_s.at[turn], field_r.at[turn]
            )
        pending.append(
            bytes_of(held.at[turn, pl.ds(1, nkp - 1)], field_s.at[turn], field_r.at[turn])
        )
        mark(f"scalars{turn}")
        if turn == 0:
            small[3].wait()
            first_beta = jnp.zeros((rows, 1), f32)
            for v in range(nv):
                first_beta = jnp.where(row_v[:, :1] == v, beta_in[0:1, v : v + 1], first_beta)
            evv, ve = take_sums(0, 2)
            sigma = evv - first_beta * ve
            base = levels * vec - first_beta * early - sigma * vec
            unit = None
            left_copy.wait()
        else:
            uv, uu, vv, euu, euv, evv = take_sums(turn, 6)
            gamma, beta = scalars(uv, uu, vv, sigma)
            coef = jnp.where(lane == turn - 1, gamma + sigma, coef)
            coef = jnp.where(lane == STEPS + turn - 1, beta, coef)
            unit = 1.0 / beta
            sigma = (euu - 2.0 * gamma * euv + gamma * gamma * evv) * unit * unit - (uv - gamma * vv)
            early = vec
            vec = (x - gamma * vec) * unit
            ratio = gamma * unit
            base = levels * vec - beta * early - sigma * vec + ratio * image
        mark(f"fieldwait{turn}")
        arrived(fields.at[turn, pl.ds(1, nkp - 1)], field_s.at[turn], field_r.at[turn])
        mark(f"left{turn}")
        field = out[:rows]
        for i in range(1, nkp):
            field = field + fields[turn, i].astype(f32)
        field = field.astype(bf16)
        part = jnp.zeros((rows, bands), f32)
        for k in range(kl):
            res = lax.dot_general(
                field, left[k], (((1,), (1,)), ((), ())), preferred_element_type=f32
            )
            part = jnp.where(row_c == k, res, part)
        shared = directs.at[turn]
        shared[0] = part.astype(bf16)
        for j in range(npw - 1, 0, -1):
            send(shared.at[0], shared.at[j], 0, j, direct_s.at[turn], direct_r.at[turn])
        pending.append(
            bytes_of(shared.at[pl.ds(1, npw - 1)], direct_s.at[turn], direct_r.at[turn])
        )
        mark(f"dirwait{turn}")
        arrived(shared.at[pl.ds(1, npw - 1)], direct_s.at[turn], direct_r.at[turn])
        mark(f"applied{turn}")
        direct = sum(shared[partner(pme, s, npw)].astype(f32) for s in range(npw))
        if turn == 0:
            image = direct
            x = base - direct
        else:
            image = direct * unit - ratio * image
            x = base - direct * unit
    mark("final")
    share_sums(STEPS, [x * vec, x * x, vec * vec])
    owns = []
    for source in (x, vec):
        own = jnp.zeros((rows, width), f32)
        for m in range(npw):
            own = jnp.where(pme == m, source[:, m * width : (m + 1) * width], own)
        owns.append(own)
    mark("finalwait")
    uv, uu, vv = take_sums(STEPS, 3)
    mark("finalout")
    gamma, beta = scalars(uv, uu, vv, sigma)
    coef = jnp.where(lane == STEPS - 1, gamma + sigma, coef)
    coef = jnp.where(lane == 2 * STEPS - 1, beta, coef)
    result_ref[0, :, :width] = (owns[0] - gamma * owns[1]) / beta
    result_ref[1, :, :width] = owns[1]
    result_ref[2] = coef
    mark("pending")
    for copy in pending:
        copy.wait_send()
    mark(None)


def unpack(result_ref, last_ref, prior_ref, alphas_ref, betas_ref):
    nv, kl, width = last_ref.shape
    for v in range(nv):
        last_ref[v] = result_ref[0, v * kl : (v + 1) * kl, :width]
        prior_ref[v] = result_ref[1, v * kl : (v + 1) * kl, :width]
        alphas_ref[v : v + 1, :] = result_ref[2, v * kl : v * kl + 1, :STEPS]
        betas_ref[v : v + 1, :] = result_ref[2, v * kl : v * kl + 1, STEPS : 2 * STEPS]


def on_device(
    nkp, npw,
    energies, current, previous, previous_beta, pair_left, pair_right, screened, momentum_index
):
    nv, kl, width = current.shape
    bands = pair_left.shape[1]
    gs = pair_left.shape[2]
    qcount = screened.shape[0]
    rows = kl * nv
    total = rows * nkp
    f32, bf16 = jnp.float32, jnp.bfloat16
    vmem = pl.BlockSpec(memory_space=pltpu.VMEM)
    hbm = pl.BlockSpec(memory_space=pltpu.HBM)
    dma = pltpu.SemaphoreType.DMA
    result = pl.pallas_call(
        functools.partial(kernel, (nkp, npw, kl, nv, bands, gs)),
        out_shape=jax.ShapeDtypeStruct((3, rows, LANES), f32),
        in_specs=[hbm] * 8,
        out_specs=vmem,
        scratch_shapes=[
            pltpu.VMEM(energies.shape, f32),
            pltpu.VMEM(current.shape, f32),
            pltpu.VMEM(current.shape, f32),
            pltpu.VMEM((1, nv), f32),
            pltpu.VMEM(momentum_index.shape, jnp.int32),
            pltpu.VMEM((kl, bands, gs), bf16),
            pltpu.VMEM((kl, bands, gs), bf16),
            pltpu.VMEM((npw, qcount, gs, gs), bf16),
            pltpu.VMEM((npw, rows, LANES), bf16),
            pltpu.VMEM((npw, 3 * rows, LANES), f32),
            pltpu.VMEM((STEPS, npw * nkp, rows, gs), bf16),
            pltpu.VMEM((STEPS, nkp, rows, gs), bf16),
            pltpu.VMEM((STEPS, nkp, rows, gs), bf16),
            pltpu.VMEM((STEPS, npw, rows, bands), bf16),
            pltpu.VMEM((STEPS + 1, nkp, rows, LANES), f32),
            pltpu.VMEM((total, 2 * qcount * total), bf16),
            pltpu.VMEM((qcount * total, gs), f32),
            dma((5,)), dma, dma, dma((npw,)),
            dma, dma, dma, dma,
            dma((STEPS,)), dma((STEPS, npw // 2)), dma((STEPS, npw)),
            dma((STEPS,)), dma((STEPS,)),
            dma((STEPS,)), dma((STEPS,)),
            dma((STEPS + 1,)), dma((STEPS + 1,)),
        ],
        compiler_params=pltpu.CompilerParams(
            collective_id=0, has_side_effects=True, vmem_limit_bytes=60 * 1024 * 1024
        ),
    )(
        energies, current, previous, previous_beta[None], momentum_index,
        pair_right, pair_left, screened,
    )
    return pl.pallas_call(
        unpack,
        out_shape=(
            jax.ShapeDtypeStruct(current.shape, f32),
            jax.ShapeDtypeStruct(current.shape, f32),
            jax.ShapeDtypeStruct((nv, STEPS), f32),
            jax.ShapeDtypeStruct((nv, STEPS), f32),
        ),
        in_specs=[vmem],
        out_specs=(vmem, vmem, vmem, vmem),
    )(result)


def solution(mesh):
    return jax.shard_map(
        functools.partial(on_device, mesh.shape["kpt"], mesh.shape["pw"]),
        mesh=mesh,
        in_specs=(
            P("kpt", "pw"),
            P(None, "kpt", "pw"),
            P(None, "kpt", "pw"),
            P(),
            P("kpt", None, "pw"),
            P("kpt", None, "pw"),
            P("kpt", "pw", None),
            P(),
        ),
        out_specs=(P(None, "kpt", "pw"), P(None, "kpt", "pw"), P(), P()),
        check_vma=False,
    )
```

time: 81.1 us -> 70.3 us (0.87)
  Pallas kernels: 75.2 us -> 69.4 us
  local copies, waits for them, and re-layouts: 4.95 us -> 0 us
    pallas_call x1, Pallas kernels: 75.2 us -> 68.1 us  [on_device(): pl.pallas_call(functools.partial(kernel, (nkp, npw, kl, nv, bands, gs)),...]
    unnamed x4 -> x0, local copies, waits for them, and re-layouts: 4.95 us -> none
    pallas_call x0 -> x1, Pallas kernels: none -> 1.34 us  [on_device(): pl.pallas_call(unpack, out_shape=(jax.ShapeDtypeStruct(current.shape, f32...]
where the time goes in v1:
time: 70.3 us; the launch traced here: 70 us
  Pallas kernels  69.4 us (99%)
    pallas_call x1, Pallas kernels, on_device(): pl.pallas_call(functools.partial(kernel, (nkp, npw, kl, nv, bands, gs)),...  68.1 us

profile of v1, /device:TPU:0, one launch (start us, length us, event | category | flops | bytes accessed | tf_op | source)
XLA Modules:
  0.0 70.0 jit_solution(14804137287874484083)
XLA Ops:
  0.6 68.1 %shard_map.111.result_ref = f32[3,8,128]{2,1,0:T(8,128)} custom-call(f32[4,64]{1,0:T(4,128)} %energies_hbm.1, f32[2,4,64]{2,1,0:T(4,128)} %current_hbm.1, f32[2,4,64]{2,1,0:T(4,128)} %previous_hbm.1, f32[1,2]{1,0:T(1,128)} %bitcast.1, s32[16,16]{1,0:T(8,128)} %index_hbm.1, bf16[4,512,512]{2,1,0:T(8,128)(2,1)} %right_hbm.1, bf16[4,512,512]{2,1,0:T(8,128)(2,1)} %left_hbm.1, ...), custom_call_target="tpu_custom_call" | custom-call | tf_op jit(solution)/shard_map/pallas_call | solution.py:387
  68.7 1.3 %shard_map.112 = (f32[2,4,64]{2,1,0:T(4,128)}, f32[2,4,64]{2,1,0:T(4,128)}, f32[2,3]{1,0:T(2,128)}, f32[2,3]{1,0:T(2,128)}) custom-call(f32[3,8,128]{2,1,0:T(8,128)} %shard_map.111.result_ref), custom_call_target="tpu_custom_call" | custom-call | tf_op jit(solution)/shard_map/pallas_call | solution.py:424
